TPU v7x, 32 devices: a whole 2x2x4 slice. The times are simulated.
32 devices in a mesh: kx: 4 (over z), ky: 4 (over y, x), kz: 2 (over core).
Axes of the slice: x: 2, y: 2, z: 4, core: 2. Of those that a mesh axis runs over, the one named last changes fastest.
Arguments:
- u_start: float32 [4, 4, 8, 2, 128, 128], P('kx', 'ky', 'kz'), may hold values from -1 to 1, as said below
- intersections: float32 [4, 4, 8, 12, 2, 128, 128], P('kx', 'ky', 'kz'), may hold values from -1.2 to 1.2, as said below
Outputs:
- u_final: float32 [4, 4, 8, 2, 128, 128], P('kx', 'ky', 'kz')
- centres: float32 [3, 3, 128], replicated
- spreads: float32 [3, 128], replicated
Inputs may be any that keep to these rules, and one draw needn't show every extreme that they name: `u_start`: each U(k) is unitary up to float32 rounding and close to the identity: every diagonal entry of U(k) has magnitude 0.7 or more. `intersections`: every diagonal entry of every M(k,b) has magnitude 0.45 or more and a phase within 1.9 of zero.
All inputs are finite; a program needn't handle non-finite values.
Results may differ from a plain program's by a relative error of at most 0.0003.
Values sent between devices are 32-bit elements; how exact they have to be, the bound alone decides.
A program may use at most 128 MiB of HBM per device.

v0:
```python
import jax
import jax.numpy as jnp
from jax import lax
from jax.sharding import PartitionSpec as P

ITERS = 3


OFFSETS = (
    (1, 1, 0),
    (1, -1, 0),
    (-1, 1, 0),
    (-1, -1, 0),
    (1, 0, 1),
    (1, 0, -1),
    (-1, 0, 1),
    (-1, 0, -1),
    (0, 1, 1),
    (0, 1, -1),
    (0, -1, 1),
    (0, -1, -1),
)
WEIGHT = 0.125
STEP_SIZE = 0.35
PRECISE = lax.Precision.HIGHEST


def extended(cells, sides, width):
    for axis, dim in sides:
        count = lax.axis_size(axis)
        head = lax.slice_in_dim(cells, 0, width, axis=dim)
        tail = lax.slice_in_dim(cells, cells.shape[dim] - width, cells.shape[dim], axis=dim)
        cells = jnp.concatenate(
            [
                lax.ppermute(tail, axis, [(i, (i + 1) % count) for i in range(count)]),
                cells,
                lax.ppermute(head, axis, [((i + 1) % count, i) for i in range(count)]),
            ],
            axis=dim,
        )
    return cells


def matmul(left, right):
    return jnp.einsum("...ij,...jk->...ik", left, right, precision=PRECISE)


def adjoint_product(left, right):
    return jnp.einsum("...ji,...jk->...ik", left, right, precision=PRECISE)


def complex_product(left_real, left_imag, right_real, right_imag):
    return (
        matmul(left_real, right_real) - matmul(left_imag, right_imag),
        matmul(left_real, right_imag) + matmul(left_imag, right_real),
    )


def gather_neighbours(unitary):
    extent_x = unitary.shape[0]
    extent_y = unitary.shape[1]
    extent_z = unitary.shape[2]
    padded = extended(unitary, (("kx", 0), ("ky", 1), ("kz", 2)), 1)
    pieces = []
    for offset in OFFSETS:
        pieces.append(
            padded[
                1 + offset[0] : 1 + offset[0] + extent_x,
                1 + offset[1] : 1 + offset[1] + extent_y,
                1 + offset[2] : 1 + offset[2] + extent_z,
            ]
        )
    return jnp.stack(pieces, axis=3)


def body(u_start, intersections):
    count_x = u_start.shape[0]
    count_y = u_start.shape[1]
    count_z = u_start.shape[2]
    width = u_start.shape[-1]
    total_points = (
        count_x
        * count_y
        * count_z
        * lax.axis_size("kx")
        * lax.axis_size("ky")
        * lax.axis_size("kz")
    )
    offset_table = jnp.array(OFFSETS, jnp.float32)
    identity = jnp.eye(width, dtype=jnp.float32)
    intersection_real = intersections[:, :, :, :, 0]
    intersection_imag = intersections[:, :, :, :, 1]
    unitary = u_start
    centre_list = []
    spread_list = []
    for iteration in range(ITERS):
        local_real = unitary[:, :, :, None, 0]
        local_imag = unitary[:, :, :, None, 1]
        left_real = adjoint_product(local_real, intersection_real) + adjoint_product(
            local_imag, intersection_imag
        )
        left_imag = adjoint_product(local_real, intersection_imag) - adjoint_product(
            local_imag, intersection_real
        )
        nearby = gather_neighbours(unitary)
        turned_real, turned_imag = complex_product(
            left_real, left_imag, nearby[:, :, :, :, 0], nearby[:, :, :, :, 1]
        )
        diagonal_real = jnp.diagonal(turned_real, axis1=-2, axis2=-1)
        diagonal_imag = jnp.diagonal(turned_imag, axis1=-2, axis2=-1)
        phases = jnp.arctan2(diagonal_imag, diagonal_real)
        magnitude = diagonal_real * diagonal_real + diagonal_imag * diagonal_imag
        first_sums = WEIGHT * jnp.einsum("xyzbn,bc->cn", phases, offset_table, precision=PRECISE)
        second_sums = WEIGHT * jnp.sum(1.0 - magnitude + phases * phases, axis=(0, 1, 2, 3))
        product_real = (
            turned_real * diagonal_real[..., None, :] + turned_imag * diagonal_imag[..., None, :]
        )
        product_imag = (
            turned_imag * diagonal_real[..., None, :] - turned_real * diagonal_imag[..., None, :]
        )
        first_total, second_total = lax.psum((first_sums, second_sums), ("kx", "ky", "kz"))
        centres = -first_total / total_points
        spreads = second_total / total_points - jnp.sum(centres * centres, axis=0)
        centre_list.append(centres)
        spread_list.append(spreads)
        shifted = phases + jnp.einsum("bc,cn->bn", offset_table, centres, precision=PRECISE)
        scaled = (shifted / magnitude)[..., None, :]
        summed_real = jnp.sum(product_real - product_imag * scaled, axis=3)
        summed_imag = jnp.sum(product_imag + product_real * scaled, axis=3)
        gradient_real = 2.0 * WEIGHT * (summed_real - jnp.swapaxes(summed_real, -1, -2))
        gradient_imag = 2.0 * WEIGHT * (summed_imag + jnp.swapaxes(summed_imag, -1, -2))
        change_real = STEP_SIZE * gradient_real
        change_imag = STEP_SIZE * gradient_imag
        inner_real = 0.5 * identity + change_real / 6.0
        inner_imag = change_imag / 6.0
        middle_real, middle_imag = complex_product(change_real, change_imag, inner_real, inner_imag)
        middle_real = identity + middle_real
        exponent_real, exponent_imag = complex_product(
            change_real, change_imag, middle_real, middle_imag
        )
        exponent_real = identity + exponent_real
        update_real, update_imag = complex_product(
            unitary[:, :, :, 0], unitary[:, :, :, 1], exponent_real, exponent_imag
        )
        unitary = jnp.stack([update_real, update_imag], axis=3)
    return (unitary, jnp.stack(centre_list), jnp.stack(spread_list))


def solution(mesh):
    in_specs = (P("kx", "ky", "kz", None, None, None), P("kx", "ky", "kz", None, None, None, None))
    out_specs = (P("kx", "ky", "kz", None, None, None), P(), P())
    return jax.shard_map(body, mesh=mesh, in_specs=in_specs, out_specs=out_specs, check_vma=False)
```

profile of v0, /device:TPU:0, one launch (start us, length us, event | category | flops | bytes accessed | tf_op | source)
XLA Modules:
  0.0 661.2 jit_solution(17291030890249032201)
XLA Ops:
  1.8 3.1 collective-permute-start
  4.9 2.1 collective-permute-start.1
  7.0 12.8 %collective-permute-done = f32[1,1,4,2,128,128]{5,4,2,3,1,0:T(8,128)S(1)} collective-permute-done((f32[1,1,4,2,128,128]{5,4,2,3,1,0:T(8,128)S(1)}, f32[1,1,4,2,128,128]{5,4,2,3,1,0:T(8,128)S(1)}, u32[]{:S(2)}, u32[]{:S(2)}) %collective-permute-start) | collective-permute-done | bytes 524320 | tf_op jit(solution)/shard_map/ppermute | solution.py:35
  20.9 8.7 %collective-permute-done.1 = f32[1,1,4,2,128,128]{5,4,2,3,1,0:T(8,128)S(1)} collective-permute-done((f32[1,1,4,2,128,128]{5,4,2,3,1,0:T(8,128)S(1)}, f32[1,1,4,2,128,128]{5,4,2,3,1,0:T(8,128)S(1)}, u32[]{:S(2)}, u32[]{:S(2)}) %collective-permute-start.1) | collective-permute-done | bytes 524320 | tf_op jit(solution)/shard_map/ppermute | solution.py:37
  32.5 7.0 %fusion.10 = f32[4,12,128,128]{3,2,1,0:T(8,128)S(1)} fusion(f32[1,1,4,12,2,128,128]{6,5,4,3,2,1,0:T(8,128)} %param.4, f32[1,1,4,2,128,128]{5,4,3,2,1,0:T(8,128)S(1)} %copy-done.1), kind=kOutput, calls=%fused_computation.22 | convolution fusion | flops 1207959552 | bytes 6553600 | tf_op jit(solution)/shard_map/...ji,...jk->...ik/dot_general | solution.py:49
  39.6 5.1 fusion.8
  44.7 5.2 fusion.94
  49.9 5.1 fusion.97
  55.0 12.8 %collective-permute-done.3 = f32[3,1,4,2,128,128]{5,4,2,3,1,0:T(8,128)S(1)} collective-permute-done((f32[3,1,4,2,128,128]{5,4,2,3,1,0:T(8,128)S(1)}, f32[3,1,4,2,128,128]{5,4,2,3,1,0:T(8,128)S(1)}, u32[]{:S(2)}, u32[]{:S(2)}) %collective-permute-start.3) | collective-permute-done | bytes 1572896 | tf_op jit(solution)/shard_map/ppermute | solution.py:35
  67.8 32.2 %collective-permute-done.2 = f32[3,1,4,2,128,128]{5,4,2,3,1,0:T(8,128)S(1)} collective-permute-done((f32[3,1,4,2,128,128]{5,4,2,3,1,0:T(8,128)S(1)}, f32[3,1,4,2,128,128]{5,4,2,3,1,0:T(8,128)S(1)}, u32[]{:S(2)}, u32[]{:S(2)}) %collective-permute-start.2) | collective-permute-done | bytes 1572896 | tf_op jit(solution)/shard_map/ppermute | solution.py:37
  101.1 2.1 collective-permute-done.4
  103.2 1.6 collective-permute-done.5
  105.2 5.7 fusion.40
  110.9 5.5 fusion.42
  116.3 6.0 fusion.71
  122.4 7.2 %fusion.68 = f32[4,12,128,128]{3,2,1,0:T(8,128)} fusion(f32[4,12,128,128]{3,2,1,0:T(8,128)S(1)} %fusion.42, f32[1,1,4,12,2,128,128]{6,5,3,2,4,1,0:T(8,128)S(1)} %fusion.152, f32[4,12,128,128]{3,2,1,0:T(8,128)S(1)} %fusion.94), kind=kOutput, calls=%fused_computation.92 | convolution fusion | flops 1208745984 | bytes 12582912 | tf_op jit(solution)/shard_map/...ij,...jk->...ik/dot_general | solution.py:45
  129.6 18.5 %copy.238 = f32[4,12,128,128]{1,0,3,2:T(4,128)} copy(f32[4,12,128,128]{3,2,1,0:T(8,128)} %fusion.68) | data formatting | bytes 6291456 | tf_op jit(solution)/shard_map/sub | solution.py:54
  148.1 1.9 gather_fusion
  151.4 16.8 %copy.243 = f32[4,12,128,128]{1,0,3,2:T(4,128)} copy(f32[4,12,128,128]{3,2,1,0:T(8,128)S(1)} %fusion.71) | data formatting | bytes 6291456 | tf_op jit(solution)/shard_map/add | solution.py:55
  168.2 1.9 gather_fusion.1
  173.0 39.8 %psum.42 = f32[3,128]{1,0:T(4,128)S(1)} all-reduce(f32[3,128]{1,0:T(4,128)} %fusion.122), channel_id=1, replica_groups=mesh['kx'=4,'ky'=4,'kz'=2] {'kx','ky','kz'}, use_global_device_ids=true, to_apply=%region_1.2 | all-reduce | flops 384 | bytes 3072 | tf_op jit(solution)/shard_map/psum | solution.py:121
  215.0 4.2 add_reduce_fusion.2
  226.5 1.6 collective-permute-start.7
  228.6 12.7 %collective-permute-done.7 = f32[1,1,4,2,128,128]{4,5,2,3,1,0:T(8,128)S(1)} collective-permute-done((f32[1,1,4,2,128,128]{4,5,2,3,1,0:T(8,128)S(1)}, f32[1,1,4,2,128,128]{4,5,2,3,1,0:T(8,128)S(1)}, u32[]{:S(2)}, u32[]{:S(2)}) %collective-permute-start.7) | collective-permute-done | bytes 524320 | tf_op jit(solution)/shard_map/ppermute | solution.py:37
  241.3 9.3 %collective-permute-done.6 = f32[1,1,4,2,128,128]{4,5,2,3,1,0:T(8,128)S(1)} collective-permute-done((f32[1,1,4,2,128,128]{4,5,2,3,1,0:T(8,128)S(1)}, f32[1,1,4,2,128,128]{4,5,2,3,1,0:T(8,128)S(1)}, u32[]{:S(2)}, u32[]{:S(2)}) %collective-permute-start.6) | collective-permute-done | bytes 524320 | tf_op jit(solution)/shard_map/ppermute | solution.py:35
  250.8 2.3 collective-permute-start.9
  254.0 3.0 fusion.6
  257.0 3.0 fusion.4
  260.0 3.0 fusion.100
  263.1 26.0 %collective-permute-done.9 = f32[3,1,4,2,128,128]{4,5,2,3,1,0:T(8,128)S(1)} collective-permute-done((f32[3,1,4,2,128,128]{4,5,2,3,1,0:T(8,128)S(1)}, f32[3,1,4,2,128,128]{4,5,2,3,1,0:T(8,128)S(1)}, u32[]{:S(2)}, u32[]{:S(2)}) %collective-permute-start.9) | collective-permute-done | bytes 1572896 | tf_op jit(solution)/shard_map/ppermute | solution.py:35
  289.1 31.8 %collective-permute-done.8 = f32[3,1,4,2,128,128]{4,5,2,3,1,0:T(8,128)S(1)} collective-permute-done((f32[3,1,4,2,128,128]{4,5,2,3,1,0:T(8,128)S(1)}, f32[3,1,4,2,128,128]{4,5,2,3,1,0:T(8,128)S(1)}, u32[]{:S(2)}, u32[]{:S(2)}) %collective-permute-start.8) | collective-permute-done | bytes 1572896 | tf_op jit(solution)/shard_map/ppermute | solution.py:37
  321.6 3.0 fusion.103
  327.2 6.8 %fusion.34 = f32[4,12,128,128]{3,2,1,0:T(8,128)S(1)} fusion(f32[4,128,12,128]{3,1,2,0:T(8,128)S(1)} %fusion.103, f32[4,12,128,128]{2,3,0,1:T(8,128)S(1)} %get-tuple-element.33), kind=kOutput, calls=%fused_computation.46 | convolution fusion | flops 1207959552 | bytes 9437184 | tf_op jit(solution)/shard_map/...ij,...jk->...ik/dot_general | solution.py:45
  334.0 6.7 %fusion.32 = f32[4,12,128,128]{3,2,1,0:T(8,128)S(1)} fusion(f32[4,128,12,128]{3,1,2,0:T(8,128)S(1)} %fusion.103, f32[4,12,128,128]{2,3,0,1:T(8,128)S(1)} %get-tuple-element.34), kind=kOutput, calls=%fused_computation.44 | convolution fusion | flops 1207959552 | bytes 9437184 | tf_op jit(solution)/shard_map/...ij,...jk->...ik/dot_general | solution.py:45
  340.7 8.6 %fusion.74 = f32[4,12,128,128]{3,2,1,0:T(8,128)} fusion(f32[4,12,128,128]{3,2,1,0:T(8,128)S(1)} %fusion.34, f32[4,12,128,128]{2,3,0,1:T(8,128)S(1)} %get-tuple-element.34, f32[4,128,12,128]{3,1,2,0:T(8,128)S(1)} %fusion.100), kind=kOutput, calls=%fused_computation.94 | convolution fusion | flops 1208745984 | bytes 12582912 | tf_op jit(solution)/shard_map/...ij,...jk->...ik/dot_general | solution.py:45
  349.3 8.4 %fusion.79 = f32[4,12,128,128]{3,2,1,0:T(8,128)} fusion(f32[4,12,128,128]{3,2,1,0:T(8,128)S(1)} %fusion.32, f32[4,12,128,128]{2,3,0,1:T(8,128)S(1)} %get-tuple-element.33, f32[4,128,12,128]{3,1,2,0:T(8,128)S(1)} %fusion.100), kind=kOutput, calls=%fused_computation.95 | convolution fusion | flops 1208745984 | bytes 12582912 | tf_op jit(solution)/shard_map/...ij,...jk->...ik/dot_general | solution.py:45
  357.6 18.5 %copy.266 = f32[4,12,128,128]{1,0,3,2:T(4,128)} copy(f32[4,12,128,128]{3,2,1,0:T(8,128)} %fusion.79) | data formatting | bytes 6291456 | tf_op jit(solution)/shard_map/add | solution.py:55
  376.2 1.9 gather_fusion.3
  378.3 18.5 %copy.261 = f32[4,12,128,128]{1,0,3,2:T(4,128)} copy(f32[4,12,128,128]{3,2,1,0:T(8,128)} %fusion.74) | data formatting | bytes 6291456 | tf_op jit(solution)/shard_map/sub | solution.py:54
  396.8 1.9 gather_fusion.2
  399.2 39.5 %psum.43 = f32[3,128]{1,0:T(4,128)S(1)} all-reduce(f32[3,128]{1,0:T(4,128)S(1)} %fusion.121), channel_id=1, replica_groups=mesh['kx'=4,'ky'=4,'kz'=2] {'kx','ky','kz'}, use_global_device_ids=true, to_apply=%region_5.6 | all-reduce | flops 384 | bytes 3072 | tf_op jit(solution)/shard_map/psum | solution.py:121
  439.0 4.4 add_reduce_fusion.1
  449.9 2.3 collective-permute-start.13
  452.2 12.3 %collective-permute-done.13 = f32[1,1,4,2,128,128]{5,4,2,3,1,0:T(8,128)S(1)} collective-permute-done((f32[1,1,4,2,128,128]{5,4,2,3,1,0:T(8,128)S(1)}, f32[1,1,4,2,128,128]{5,4,2,3,1,0:T(8,128)S(1)}, u32[]{:S(2)}, u32[]{:S(2)}) %collective-permute-start.13) | collective-permute-done | bytes 524320 | tf_op jit(solution)/shard_map/ppermute | solution.py:37
  464.5 10.0 %collective-permute-done.12 = f32[1,1,4,2,128,128]{5,4,2,3,1,0:T(8,128)S(1)} collective-permute-done((f32[1,1,4,2,128,128]{5,4,2,3,1,0:T(8,128)S(1)}, f32[1,1,4,2,128,128]{5,4,2,3,1,0:T(8,128)S(1)}, u32[]{:S(2)}, u32[]{:S(2)}) %collective-permute-start.12) | collective-permute-done | bytes 524320 | tf_op jit(solution)/shard_map/ppermute | solution.py:35
  476.1 2.0 collective-permute-start.14
  478.1 3.0 fusion
  481.1 3.0 fusion.2
  484.1 3.1 fusion.109
  487.2 3.1 fusion.106
  490.3 22.6 %collective-permute-done.15 = f32[3,1,4,2,128,128]{5,4,2,3,1,0:T(8,128)S(1)} collective-permute-done((f32[3,1,4,2,128,128]{5,4,2,3,1,0:T(8,128)S(1)}, f32[3,1,4,2,128,128]{5,4,2,3,1,0:T(8,128)S(1)}, u32[]{:S(2)}, u32[]{:S(2)}) %collective-permute-start.15) | collective-permute-done | bytes 1572896 | tf_op jit(solution)/shard_map/ppermute | solution.py:35
  512.9 30.0 %collective-permute-done.14 = f32[3,1,4,2,128,128]{5,4,2,3,1,0:T(8,128)S(1)} collective-permute-done((f32[3,1,4,2,128,128]{5,4,2,3,1,0:T(8,128)S(1)}, f32[3,1,4,2,128,128]{5,4,2,3,1,0:T(8,128)S(1)}, u32[]{:S(2)}, u32[]{:S(2)}) %collective-permute-start.14) | collective-permute-done | bytes 1572896 | tf_op jit(solution)/shard_map/ppermute | solution.py:37
  544.1 2.0 collective-permute-done.16
  546.1 1.6 collective-permute-done.17
  548.9 3.9 fusion.26
  552.8 3.5 fusion.24
  556.3 5.3 fusion.84
  561.6 5.3 fusion.89
  566.9 18.5 %copy.294 = f32[4,12,128,128]{1,0,3,2:T(4,128)} copy(f32[4,12,128,128]{3,2,1,0:T(8,128)} %fusion.89) | data formatting | bytes 6291456 | tf_op jit(solution)/shard_map/add | solution.py:55
  585.4 1.9 gather_fusion.5
  587.4 18.5 %copy.289 = f32[4,12,128,128]{1,0,3,2:T(4,128)} copy(f32[4,12,128,128]{3,2,1,0:T(8,128)} %fusion.84) | data formatting | bytes 6291456 | tf_op jit(solution)/shard_map/sub | solution.py:54
  605.9 1.9 gather_fusion.4
  608.3 39.9 %all-reduce = (f32[3,128]{1,0:T(4,128)S(1)}, f32[128]{0:T(128)S(1)}, f32[128]{0:T(128)S(1)}, f32[128]{0:T(128)S(1)}) all-reduce(f32[3,128]{1,0:T(4,128)S(1)} %fusion.120, f32[128]{0:T(128)S(1)} %broadcast_multiply_fusion, f32[128]{0:T(128)S(1)} %broadcast_multiply_fusion.1, ...), channel_id=1, replica_groups=mesh['kx'=4,'ky'=4,'kz'=2] {'kx','ky','kz'}, use_global_device_ids=true, to_apply=%region_9.10 | all-reduce | flops 768 | bytes 6144 | tf_op jit(solution)/shard_map/psum | solution.py:121
  648.7 4.5 subtract_reduce_fusion
  (178 shorter events, 44.8 us)
Async XLA Ops:
  0.6 31.9 %copy-start.1 = (f32[1,1,4,2,128,128]{5,4,3,2,1,0:T(8,128)S(1)}, f32[1,1,4,2,128,128]{5,4,3,2,1,0:T(8,128)}, u32[]{:S(2)}) copy-start(f32[1,1,4,2,128,128]{5,4,3,2,1,0:T(8,128)} %param.3) | copy-start | bytes 1572868
  1.8 17.9 %collective-permute-start = (f32[1,1,4,2,128,128]{5,4,2,3,1,0:T(8,128)S(1)}, f32[1,1,4,2,128,128]{5,4,2,3,1,0:T(8,128)S(1)}, u32[]{:S(2)}, u32[]{:S(2)}) collective-permute-start(f32[1,1,4,2,128,128]{5,4,2,3,1,0:T(8,128)S(1)} %copy.219), channel_id=1, source_target_pairs={{0,8},{8,16},{16,24},{24,0},{1,9},{9,17},{17,25},{25,1},{2,10},{10... | collective-permute-start | bytes 1572872 | tf_op jit(solution)/shard_map/ppermute | solution.py:35
  4.9 24.6 %collective-permute-start.1 = (f32[1,1,4,2,128,128]{5,4,2,3,1,0:T(8,128)S(1)}, f32[1,1,4,2,128,128]{5,4,2,3,1,0:T(8,128)S(1)}, u32[]{:S(2)}, u32[]{:S(2)}) collective-permute-start(f32[1,1,4,2,128,128]{5,4,2,3,1,0:T(8,128)S(1)} %copy.219), channel_id=1, source_target_pairs={{8,0},{16,8},{24,16},{0,24},{9,1},{17,9},{25,17},{1,25},{10,2},{18... | collective-permute-start | bytes 1572872 | tf_op jit(solution)/shard_map/ppermute | solution.py:37
  29.6 10.1 %copy-start = (f32[1,1,4,12,2,128,128]{6,5,4,3,2,1,0:T(8,128)S(1)}, f32[1,1,4,12,2,128,128]{6,5,4,3,2,1,0:T(8,128)}, u32[]{:S(2)}) copy-start(f32[1,1,4,12,2,128,128]{6,5,4,3,2,1,0:T(8,128)} %param.4) | copy-start | bytes 18874372
  29.6 38.2 %collective-permute-start.3 = (f32[3,1,4,2,128,128]{5,4,2,3,1,0:T(8,128)S(1)}, f32[3,1,4,2,128,128]{5,4,2,3,1,0:T(8,128)S(1)}, u32[]{:S(2)}, u32[]{:S(2)}) collective-permute-start(f32[3,1,4,2,128,128]{5,4,2,3,1,0:T(8,128)S(1)} %constant_dynamic-update-slice_fusion), channel_id=1, source_target_pairs={{0,2},{2,4},{4,6},{6,0},{1,3},{3,5},{5,7},{7,1},{8,10},{10,12},{12... | collective-permute-start | bytes 4718600 | tf_op jit(solution)/shard_map/ppermute | solution.py:35
  31.1 68.9 %collective-permute-start.2 = (f32[3,1,4,2,128,128]{5,4,2,3,1,0:T(8,128)S(1)}, f32[3,1,4,2,128,128]{5,4,2,3,1,0:T(8,128)S(1)}, u32[]{:S(2)}, u32[]{:S(2)}) collective-permute-start(f32[3,1,4,2,128,128]{5,4,2,3,1,0:T(8,128)S(1)} %constant_dynamic-update-slice_fusion), channel_id=1, source_target_pairs={{2,0},{4,2},{6,4},{0,6},{3,1},{5,3},{7,5},{1,7},{10,8},{12,10},{14... | collective-permute-start | bytes 4718600 | tf_op jit(solution)/shard_map/ppermute | solution.py:37
  100.3 2.9 collective-permute-start.4
  100.4 4.5 collective-permute-start.5
  151.4 20.8 %copy-start.3 = (f32[12,3]{1,0:T(8,128)S(1)}, f32[12,3]{1,0:T(8,128)}, u32[]{:S(2)}) copy-start(f32[12,3]{1,0:T(8,128)} %constant.59.clone) | copy-start | bytes 436
  221.1 32.9 %slice-start = ((s8[6291456]{0:T(1024)(128)(4,1)}), s8[4194304]{0:T(1024)(128)(4,1)S(1)}, s32[]{:S(2)}) async-start(s8[6291456]{0:T(1024)(128)(4,1)} %bitcast.643), calls=%async_computation | async-start | bytes 8388608
  221.5 2.5 copy-start.2
  224.0 30.0 %slice-start.1 = ((s8[6291456]{0:T(1024)(128)(4,1)}), s8[2097152]{0:T(1024)(128)(4,1)S(1)}, s32[]{:S(2)}) async-start(s8[6291456]{0:T(1024)(128)(4,1)} %bitcast.643), calls=%async_computation.1 | async-start | bytes 4194304
  226.5 14.8 %collective-permute-start.7 = (f32[1,1,4,2,128,128]{4,5,2,3,1,0:T(8,128)S(1)}, f32[1,1,4,2,128,128]{4,5,2,3,1,0:T(8,128)S(1)}, u32[]{:S(2)}, u32[]{:S(2)}) collective-permute-start(f32[1,1,4,2,128,128]{4,5,2,3,1,0:T(8,128)S(1)} %pad_maximum_fusion.47), channel_id=1, source_target_pairs={{8,0},{16,8},{24,16},{0,24},{9,1},{17,9},{25,17},{1,25},{10,2},{18... | collective-permute-start | bytes 1572872 | tf_op jit(solution)/shard_map/ppermute | solution.py:37
  228.1 22.6 %collective-permute-start.6 = (f32[1,1,4,2,128,128]{4,5,2,3,1,0:T(8,128)S(1)}, f32[1,1,4,2,128,128]{4,5,2,3,1,0:T(8,128)S(1)}, u32[]{:S(2)}, u32[]{:S(2)}) collective-permute-start(f32[1,1,4,2,128,128]{4,5,2,3,1,0:T(8,128)S(1)} %pad_maximum_fusion.47), channel_id=1, source_target_pairs={{0,8},{8,16},{16,24},{24,0},{1,9},{9,17},{17,25},{25,1},{2,10},{10... | collective-permute-start | bytes 1572872 | tf_op jit(solution)/shard_map/ppermute | solution.py:35
  250.8 38.2 %collective-permute-start.9 = (f32[3,1,4,2,128,128]{4,5,2,3,1,0:T(8,128)S(1)}, f32[3,1,4,2,128,128]{4,5,2,3,1,0:T(8,128)S(1)}, u32[]{:S(2)}, u32[]{:S(2)}) collective-permute-start(f32[3,1,4,2,128,128]{4,5,2,3,1,0:T(8,128)S(1)} %pad_maximum_fusion), channel_id=1, source_target_pairs={{0,2},{2,4},{4,6},{6,0},{1,3},{3,5},{5,7},{7,1},{8,10},{10,12},{12... | collective-permute-start | bytes 4718600 | tf_op jit(solution)/shard_map/ppermute | solution.py:35
  253.2 67.6 %collective-permute-start.8 = (f32[3,1,4,2,128,128]{4,5,2,3,1,0:T(8,128)S(1)}, f32[3,1,4,2,128,128]{4,5,2,3,1,0:T(8,128)S(1)}, u32[]{:S(2)}, u32[]{:S(2)}) collective-permute-start(f32[3,1,4,2,128,128]{4,5,2,3,1,0:T(8,128)S(1)} %pad_maximum_fusion), channel_id=1, source_target_pairs={{2,0},{4,2},{6,4},{0,6},{3,1},{5,3},{7,5},{1,7},{10,8},{12,10},{14... | collective-permute-start | bytes 4718600 | tf_op jit(solution)/shard_map/ppermute | solution.py:37
  321.1 4.6 collective-permute-start.11
  321.1 4.5 collective-permute-start.10
  444.5 33.6 %slice-start.2 = ((s8[6291456]{0:T(1024)(128)(4,1)}), s8[4194304]{0:T(1024)(128)(4,1)S(1)}, s32[]{:S(2)}) async-start(s8[6291456]{0:T(1024)(128)(4,1)} %bitcast.645), calls=%async_computation.2 | async-start | bytes 8388608
  447.0 5.2 copy-start.4
  447.4 30.6 %slice-start.3 = ((s8[6291456]{0:T(1024)(128)(4,1)}), s8[2097152]{0:T(1024)(128)(4,1)S(1)}, s32[]{:S(2)}) async-start(s8[6291456]{0:T(1024)(128)(4,1)} %bitcast.645), calls=%async_computation.3 | async-start | bytes 4194304
  449.9 14.6 %collective-permute-start.13 = (f32[1,1,4,2,128,128]{5,4,2,3,1,0:T(8,128)S(1)}, f32[1,1,4,2,128,128]{5,4,2,3,1,0:T(8,128)S(1)}, u32[]{:S(2)}, u32[]{:S(2)}) collective-permute-start(f32[1,1,4,2,128,128]{5,4,2,3,1,0:T(8,128)S(1)} %pad_maximum_fusion.48), channel_id=1, source_target_pairs={{8,0},{16,8},{24,16},{0,24},{9,1},{17,9},{25,17},{1,25},{10,2},{18... | collective-permute-start | bytes 1572872 | tf_op jit(solution)/shard_map/ppermute | solution.py:37
  452.2 22.4 %collective-permute-start.12 = (f32[1,1,4,2,128,128]{5,4,2,3,1,0:T(8,128)S(1)}, f32[1,1,4,2,128,128]{5,4,2,3,1,0:T(8,128)S(1)}, u32[]{:S(2)}, u32[]{:S(2)}) collective-permute-start(f32[1,1,4,2,128,128]{5,4,2,3,1,0:T(8,128)S(1)} %pad_maximum_fusion.48), channel_id=1, source_target_pairs={{0,8},{8,16},{16,24},{24,0},{1,9},{9,17},{17,25},{25,1},{2,10},{10... | collective-permute-start | bytes 1572872 | tf_op jit(solution)/shard_map/ppermute | solution.py:35
  474.7 38.2 %collective-permute-start.15 = (f32[3,1,4,2,128,128]{5,4,2,3,1,0:T(8,128)S(1)}, f32[3,1,4,2,128,128]{5,4,2,3,1,0:T(8,128)S(1)}, u32[]{:S(2)}, u32[]{:S(2)}) collective-permute-start(f32[3,1,4,2,128,128]{5,4,2,3,1,0:T(8,128)S(1)} %pad_maximum_fusion.1), channel_id=1, source_target_pairs={{0,2},{2,4},{4,6},{6,0},{1,3},{3,5},{5,7},{7,1},{8,10},{10,12},{12... | collective-permute-start | bytes 4718600 | tf_op jit(solution)/shard_map/ppermute | solution.py:35
  476.1 66.8 %collective-permute-start.14 = (f32[3,1,4,2,128,128]{5,4,2,3,1,0:T(8,128)S(1)}, f32[3,1,4,2,128,128]{5,4,2,3,1,0:T(8,128)S(1)}, u32[]{:S(2)}, u32[]{:S(2)}) collective-permute-start(f32[3,1,4,2,128,128]{5,4,2,3,1,0:T(8,128)S(1)} %pad_maximum_fusion.1), channel_id=1, source_target_pairs={{2,0},{4,2},{6,4},{0,6},{3,1},{5,3},{7,5},{1,7},{10,8},{12,10},{14... | collective-permute-start | bytes 4718600 | tf_op jit(solution)/shard_map/ppermute | solution.py:37
  543.2 2.9 collective-permute-start.16
  543.3 4.5 collective-permute-start.17
where the time goes:
time: 672 us; the launch traced here: 661 us
  waiting for transfers between devices  229 us (34%)
  matrix products  137 us (20%)
  local copies, waits for them, and re-layouts  133 us (20%)
  blocking collectives  119 us (18%)
  starting transfers between devices  20.8 us (3%)
  other arithmetic  19.8 us (3%)
    ppermute x9, waiting for transfers between devices, extended(): lax.ppermute(head, axis, [((i + 1) % count, i) for i in range(count)])  133 us
    psum x3, blocking collectives, body(): lax.psum((first_sums, second_sums), ('kx', 'ky', 'kz'))  119 us
    ppermute x9, waiting for transfers between devices, extended(): lax.ppermute(tail, axis, [(i, (i + 1) % count) for i in range(count)])  96.8 us
    dot_general x48, matrix products, matmul(): return jnp.einsum('...ij,...jk->...ik', left, right, precision=PRECISE)  89 us
    sub x3, local copies, waits for them, and re-layouts, complex_product(): matmul(left_real, right_real) - matmul(left_imag, right_imag)  55.6 us
    add x3, local copies, waits for them, and re-layouts, complex_product(): matmul(left_real, right_imag) + matmul(left_imag, right_real)  53.8 us
    dot_general x12, matrix products, adjoint_product(): return jnp.einsum('...ji,...jk->...ik', left, right, precision=PRECISE)  46.7 us
  transfers between devices with their start and end apart: 18, of which 17 were waited for; matrix products, arithmetic and copies ran while one was open for 7% of the time, Pallas kernels for 0%

commit v1 on v0

v1 whole, which is shorter than its diff:
```python
import functools

import jax
import jax.numpy as jnp
from jax import lax
from jax.experimental import pallas as pl
from jax.experimental.pallas import tpu as pltpu
from jax.sharding import PartitionSpec as P

ITERS = 3


OFFSETS = (
    (1, 1, 0),
    (1, -1, 0),
    (-1, 1, 0),
    (-1, -1, 0),
    (1, 0, 1),
    (1, 0, -1),
    (-1, 0, 1),
    (-1, 0, -1),
    (0, 1, 1),
    (0, 1, -1),
    (0, -1, 1),
    (0, -1, -1),
)
NB = len(OFFSETS)
CORNERS = tuple(b for b in range(NB) if OFFSETS[b][2] == 0)
FACES = tuple(b for b in range(NB) if OFFSETS[b][2] != 0)
FACE_COLUMNS = ((0, -1), (0, 1), (-1, 0), (1, 0))
WEIGHT = 0.125
STEP_SIZE = 0.35
MESH = pl.DeviceIdType.MESH
F32 = jnp.float32
BF16 = jnp.bfloat16


def column(dx, dy):
    return (dx + 1) * 3 + dy + 1


def split(x):
    high = x.astype(BF16)
    return high, (x - high.astype(F32)).astype(BF16)


def left_rows(high, low):
    return jnp.concatenate([high, high, low], axis=1)


def stacked(real, imag, flip):
    rh, rl = split(real)
    ih, il = split(imag)
    if flip:
        high = jnp.concatenate(
            [jnp.concatenate([rh, ih], axis=1), jnp.concatenate([ih, -rh], axis=1)], axis=0
        )
        low = jnp.concatenate(
            [jnp.concatenate([rl, il], axis=1), jnp.concatenate([il, -rl], axis=1)], axis=0
        )
    else:
        high = jnp.concatenate(
            [jnp.concatenate([rh, ih], axis=1), jnp.concatenate([-ih, rh], axis=1)], axis=0
        )
        low = jnp.concatenate(
            [jnp.concatenate([rl, il], axis=1), jnp.concatenate([-il, rl], axis=1)], axis=0
        )
    return jnp.concatenate([high, low, high], axis=0)


def product(left, right):
    return jnp.dot(left, right, preferred_element_type=F32)


def complex_product(left, right_real, right_imag):
    return product(left_rows(*split(left)), stacked(right_real, right_imag, False))


def arctan2(y, x):
    ay = jnp.abs(y)
    ax = jnp.abs(x)
    ratio = jnp.minimum(ax, ay) / jnp.maximum(jnp.maximum(ax, ay), 1e-37)
    far = ratio > 0.4142135623730950
    z = jnp.where(far, (ratio - 1.0) / (ratio + 1.0), ratio)
    s = z * z
    poly = (
        ((8.05374449538e-2 * s - 1.38776856032e-1) * s + 1.99777106478e-1) * s - 3.33329491539e-1
    ) * s * z + z
    angle = jnp.where(far, poly + 0.7853981633974483, poly)
    angle = jnp.where(ay > ax, 1.5707963267948966 - angle, angle)
    angle = jnp.where(x < 0.0, 3.141592653589793 - angle, angle)
    return jnp.where(y < 0.0, -angle, angle)


def signed_sum(rows):
    total = None
    for sign, row in rows:
        if total is None:
            total = row if sign > 0 else -row
        else:
            total = total + row if sign > 0 else total - row
    return total


def kernel(
    sizes,
    total_points,
    u_ref,
    m_ref,
    out_ref,
    centres_ref,
    spreads_ref,
    own,
    halo,
    inter,
    rot,
    uth,
    dre,
    dim,
    gre,
    gim,
    gz,
    gy,
    gx,
    load_u,
    load_m,
    y_send,
    y_recv,
    x_send,
    x_recv,
    f_send,
    f_recv,
    gz_send,
    gz_recv,
    gy_send,
    gy_recv,
    gx_send,
    gx_recv,
):
    nx, ny, nz = sizes
    count = own.shape[1]
    width = own.shape[-1]
    mx = lax.axis_index("kx")
    my = lax.axis_index("ky")
    mz = lax.axis_index("kz")

    def at(dx, dy, dz):
        return (
            lax.rem(mx + (dx + nx), nx),
            lax.rem(my + (dy + ny), ny),
            lax.rem(mz + (dz + nz), nz),
        )

    copy_u = pltpu.make_async_copy(u_ref, own.at[0], load_u)
    copy_u.start()
    for k in range(count):
        pltpu.make_async_copy(m_ref.at[k], inter.at[k], load_m.at[k]).start()

    partners = (
        [at(j, 0, 0) for j in range(1, nx)]
        + [at(0, j, 0) for j in range(1, ny)]
        + [at(0, 0, j) for j in range(1, nz)]
    )
    barrier = pltpu.get_barrier_semaphore()
    for partner in partners:
        pl.semaphore_signal(barrier, inc=1, device_id=partner, device_id_type=MESH)
    pl.semaphore_wait(barrier, len(partners))
    copy_u.wait()

    def remote(src, dst, send, recv, target):
        return pltpu.make_async_remote_copy(
            src_ref=src,
            dst_ref=dst,
            send_sem=send,
            recv_sem=recv,
            device_id=target,
            device_id_type=MESH,
        )

    def y_copy(t, j, k):
        slot = -1 if j == 0 else 1
        return remote(
            own.at[t, k],
            halo.at[t, column(0, slot), k + 1],
            y_send.at[t, j, k],
            y_recv.at[t, j, k],
            at(0, -slot, 0),
        )

    def x_copy(t, i, dy, k):
        slot = -1 if i == 0 else 1
        src = own.at[t, k] if dy == 0 else halo.at[t, column(0, dy), k + 1]
        return remote(
            src,
            halo.at[t, column(slot, dy), k + 1],
            x_send.at[t, i, dy + 1, k],
            x_recv.at[t, i, dy + 1, k],
            at(-slot, 0, 0),
        )

    def f_copy(t, f, side):
        col = column(*FACE_COLUMNS[f])
        if side == 0:
            src, dst, target = 1, count + 1, at(0, 0, -1)
        else:
            src, dst, target = count, 0, at(0, 0, 1)
        return remote(
            halo.at[t, col, src],
            halo.at[t, col, dst],
            f_send.at[t, f, side],
            f_recv.at[t, f, side],
            target,
        )

    row_index = lax.broadcasted_iota(jnp.int32, (width, width), 0)
    column_index = lax.broadcasted_iota(jnp.int32, (width, width), 1)
    diagonal = row_index == column_index
    identity = jnp.where(diagonal, 1.0, 0.0).astype(F32)

    def all_sum(t, axis_slots, send, recv, me, size, target, value):
        axis_slots[t, me] = value
        copies = []
        for j in range(1, size):
            copies.append(
                remote(
                    axis_slots.at[t, me],
                    axis_slots.at[t, me],
                    send.at[t, j],
                    recv.at[t, j],
                    target(j),
                )
            )
            copies[-1].start()
        for j in range(1, size):
            source = lax.rem(me + (size - j), size)
            remote(
                axis_slots.at[t, source],
                axis_slots.at[t, source],
                send.at[t, j],
                recv.at[t, j],
                target(j),
            ).wait_recv()
        for copy in copies:
            copy.wait_send()
        total = axis_slots[t, 0]
        for j in range(1, size):
            total = total + axis_slots[t, j]
        return total

    def turn(t, k, b):
        dx, dy, dz = OFFSETS[b]
        left = rot[k, b]
        right = halo.at[t, column(dx, dy), k + 1 + dz]
        turned = complex_product(left, right[0], right[1])
        rot[k, b] = turned
        dre[k, b : b + 1, :] = jnp.sum(
            jnp.where(diagonal, turned[:, :width], 0.0), axis=0, keepdims=True
        )
        dim[k, b : b + 1, :] = jnp.sum(
            jnp.where(diagonal, turned[:, width:], 0.0), axis=0, keepdims=True
        )

    def iteration(t, carry):
        for k in range(count):
            for j in range(2):
                y_copy(t, j, k).start()
            for i in range(2):
                x_copy(t, i, 0, k).start()

        def left_side(k, carry):
            @pl.when(t == 0)
            def _():
                pltpu.make_async_copy(m_ref.at[k], inter.at[k], load_m.at[k]).wait()

            adjoint = jnp.concatenate([own[t, k, 0].T, own[t, k, 1].T], axis=1)
            uth[...] = left_rows(*split(adjoint))

            def one(b, carry):
                rot[k, b] = product(uth[...], stacked(inter[k, b, 0], inter[k, b, 1], True))
                return carry

            lax.fori_loop(0, NB, one, 0, unroll=3)
            for j in range(2):
                y_copy(t, j, k).wait_recv()
                for i in range(2):
                    x_copy(t, i, -1 if j == 0 else 1, k).start()
            for i in range(2):
                x_copy(t, i, 0, k).wait_recv()

            @pl.when(k == 0)
            def _():
                for f in range(4):
                    f_copy(t, f, 0).start()

            @pl.when(k == count - 1)
            def _():
                for f in range(4):
                    f_copy(t, f, 1).start()

            return carry

        lax.fori_loop(0, count, left_side, 0)
        for f in range(4):
            for side in range(2):
                f_copy(t, f, side).wait_recv()

        def faces(k, carry):
            for b in FACES:
                turn(t, k, b)
            return carry

        lax.fori_loop(0, count, faces, 0)

        def corners(k, carry):
            for i in range(2):
                for dy in (-1, 1):
                    x_copy(t, i, dy, k).wait_recv()
            for b in CORNERS:
                turn(t, k, b)
            return carry

        lax.fori_loop(0, count, corners, 0)

        real = dre[:, :NB, :]
        imag = dim[:, :NB, :]
        phases = arctan2(imag, real)
        magnitude = real * real + imag * imag
        phase_rows = jnp.sum(phases, axis=0)
        second = jnp.sum(
            jnp.sum(1.0 - magnitude + phases * phases, axis=0), axis=0, keepdims=True
        )
        rows = [
            signed_sum(
                [
                    (OFFSETS[b][c], phase_rows[b : b + 1, :])
                    for b in range(NB)
                    if OFFSETS[b][c] != 0
                ]
            )
            for c in range(3)
        ]
        packed = WEIGHT * jnp.concatenate(
            rows + [second] + [jnp.zeros((4, width), F32)], axis=0
        )
        packed = all_sum(t, gz, gz_send, gz_recv, mz, nz, lambda j: at(0, 0, j), packed)
        packed = all_sum(t, gy, gy_send, gy_recv, my, ny, lambda j: at(0, j, 0), packed)
        packed = all_sum(t, gx, gx_send, gx_recv, mx, nx, lambda j: at(j, 0, 0), packed)
        packed = packed / total_points
        centres = -packed[0:3, :]
        spread = packed[3:4, :] - jnp.sum(centres * centres, axis=0, keepdims=True)
        centres_ref[t] = centres
        spreads_ref[t] = spread
        shift = jnp.concatenate(
            [
                signed_sum(
                    [
                        (OFFSETS[b][c], centres[c : c + 1, :])
                        for c in range(3)
                        if OFFSETS[b][c] != 0
                    ]
                )
                for b in range(NB)
            ],
            axis=0,
        )
        scaled = (phases + shift[None]) / magnitude
        gre[:, :NB, :] = real + imag * scaled
        gim[:, :NB, :] = real * scaled - imag

        def update(k, carry):
            summed_real = jnp.zeros((width, width), F32)
            summed_imag = jnp.zeros((width, width), F32)
            for b in range(NB):
                turned_real = rot[k, b, :, :width]
                turned_imag = rot[k, b, :, width:]
                factor_real = gre[k, b : b + 1, :]
                factor_imag = gim[k, b : b + 1, :]
                summed_real = summed_real + (
                    turned_real * factor_real - turned_imag * factor_imag
                )
                summed_imag = summed_imag + (
                    turned_real * factor_imag + turned_imag * factor_real
                )
            scale = STEP_SIZE * 2.0 * WEIGHT
            change_real = scale * (summed_real - summed_real.T)
            change_imag = scale * (summed_imag + summed_imag.T)
            change = left_rows(*split(jnp.concatenate([change_real, change_imag], axis=1)))
            middle = product(
                change,
                stacked(0.5 * identity + change_real / 6.0, change_imag / 6.0, False),
            )
            exponent = product(
                change, stacked(identity + middle[:, :width], middle[:, width:], False)
            )
            updated = complex_product(
                jnp.concatenate([own[t, k, 0], own[t, k, 1]], axis=1),
                identity + exponent[:, :width],
                exponent[:, width:],
            )
            own[t + 1, k, 0] = updated[:, :width]
            own[t + 1, k, 1] = updated[:, width:]
            return carry

        lax.fori_loop(0, count, update, 0)

        def drain(k, carry):
            for j in range(2):
                y_copy(t, j, k).wait_send()
            for i in range(2):
                for dy in (-1, 0, 1):
                    x_copy(t, i, dy, k).wait_send()
            return carry

        lax.fori_loop(0, count, drain, 0)
        for f in range(4):
            for side in range(2):
                f_copy(t, f, side).wait_send()
        return carry

    lax.fori_loop(0, ITERS, iteration, 0)
    out_ref[...] = own[ITERS]


def body(sizes, u_start, intersections):
    nx, ny, nz = sizes
    count_x, count_y, count = u_start.shape[:3]
    width = u_start.shape[-1]
    assert count_x == 1 and count_y == 1
    total_points = count_x * count_y * count * nx * ny * nz
    dma = pltpu.SemaphoreType.DMA
    unitary, centres, spreads = pl.pallas_call(
        functools.partial(kernel, sizes, float(total_points)),
        out_shape=(
            jax.ShapeDtypeStruct((count, 2, width, width), F32),
            jax.ShapeDtypeStruct((ITERS, 3, width), F32),
            jax.ShapeDtypeStruct((ITERS, 1, width), F32),
        ),
        in_specs=[pl.BlockSpec(memory_space=pl.ANY)] * 2,
        out_specs=tuple([pl.BlockSpec(memory_space=pltpu.VMEM)] * 3),
        scratch_shapes=[
            pltpu.VMEM((ITERS + 1, count, 2, width, width), F32),
            pltpu.VMEM((ITERS, 9, count + 2, 2, width, width), F32),
            pltpu.VMEM((count, NB, 2, width, width), F32),
            pltpu.VMEM((count, NB, width, 2 * width), F32),
            pltpu.VMEM((width, 6 * width), BF16),
            pltpu.VMEM((count, 16, width), F32),
            pltpu.VMEM((count, 16, width), F32),
            pltpu.VMEM((count, 16, width), F32),
            pltpu.VMEM((count, 16, width), F32),
            pltpu.VMEM((ITERS, nz, 8, width), F32),
            pltpu.VMEM((ITERS, ny, 8, width), F32),
            pltpu.VMEM((ITERS, nx, 8, width), F32),
            dma,
            dma((count,)),
            dma((ITERS, 2, count)),
            dma((ITERS, 2, count)),
            dma((ITERS, 2, 3, count)),
            dma((ITERS, 2, 3, count)),
            dma((ITERS, 4, 2)),
            dma((ITERS, 4, 2)),
            dma((ITERS, nz)),
            dma((ITERS, nz)),
            dma((ITERS, ny)),
            dma((ITERS, ny)),
            dma((ITERS, nx)),
            dma((ITERS, nx)),
        ],
        compiler_params=pltpu.CompilerParams(
            collective_id=0, has_side_effects=True, vmem_limit_bytes=60 * 1024 * 1024
        ),
    )(
        u_start.reshape(u_start.shape[2:]),
        intersections.reshape(intersections.shape[2:]),
    )
    return unitary.reshape(u_start.shape), centres, spreads.reshape(ITERS, width)


def solution(mesh):
    sizes = (mesh.shape["kx"], mesh.shape["ky"], mesh.shape["kz"])
    in_specs = (P("kx", "ky", "kz", None, None, None), P("kx", "ky", "kz", None, None, None, None))
    out_specs = (P("kx", "ky", "kz", None, None, None), P(), P())
    return jax.shard_map(
        functools.partial(body, sizes),
        mesh=mesh,
        in_specs=in_specs,
        out_specs=out_specs,
        check_vma=False,
    )
```

time: 672 us -> 259 us (0.39); the launches traced: 661 us -> 259 us
  Pallas kernels: 0 us -> 254 us
  waiting for transfers between devices: 229 us -> 0 us
  matrix products: 137 us -> 0 us
  local copies, waits for them, and re-layouts: 133 us -> 4.41 us
  blocking collectives: 119 us -> 0 us
  starting transfers between devices: 20.8 us -> 0 us
  other arithmetic: 19.8 us -> 0 us
    pallas_call x0 -> x1, Pallas kernels: none -> 254 us  [body(): pl.pallas_call(functools.partial(kernel, sizes, float(total_points)), out...]
    ppermute x18 -> x0, waiting for transfers between devices: 229 us -> none  [the longest x9 133 us: extended(): lax.ppermute(head, axis, [((i + 1) % count, i) for i in range(count)])]
    dot_general x66 -> x0, matrix products: 137 us -> none  [the longest x48 89 us: matmul(): return jnp.einsum('...ij,...jk->...ik', left, right, precision=PRECISE)]
    psum x3 -> x0, blocking collectives: 119 us -> none  [body(): lax.psum((first_sums, second_sums), ('kx', 'ky', 'kz'))]
    sub x3 -> x0, local copies, waits for them, and re-layouts: 55.6 us -> none  [complex_product(): matmul(left_real, right_real) - matmul(left_imag, right_imag)]
    add x3 -> x0, local copies, waits for them, and re-layouts: 53.8 us -> none  [complex_product(): matmul(left_real, right_imag) + matmul(left_imag, right_real)]
    ppermute x18 -> x0, starting transfers between devices: 20.8 us -> none  [the longest x9 10.8 us: extended(): lax.ppermute(head, axis, [((i + 1) % count, i) for i in range(count)])]
    gather x18 -> x0, local copies, waits for them, and re-layouts: 15.1 us -> none  [the longest x9 7.55 us: body(): diagonal_imag = jnp.diagonal(turned_imag, axis1=-2, axis2=-1)]
  transfers between devices with their start and end apart: 18 -> 0, of which waited for: 17 -> 0; matrix products, arithmetic and copies ran while one was open for 7% -> 0% of each run, Pallas kernels for 0% -> 0%
where the time goes in v1:
time: 259 us
  Pallas kernels  254 us (98%)
  local copies, waits for them, and re-layouts  4.41 us (2%)
    pallas_call x1, Pallas kernels, body(): pl.pallas_call(functools.partial(kernel, sizes, float(total_points)), out...  254 us

profile of v1, /device:TPU:0, one launch (start us, length us, event | category | flops | bytes accessed | tf_op | source)
XLA Modules:
  0.0 258.6 jit_solution(12810583370911095089)
XLA Ops:
  0.6 253.5 %shard_map.49 = (f32[4,2,128,128]{3,2,1,0:T(8,128)}, f32[3,3,128]{2,1,0:T(4,128)}, f32[3,1,128]{2,1,0:T(1,128)}) custom-call(f32[4,2,128,128]{3,2,1,0:T(8,128)} %bitcast.8, f32[4,12,2,128,128]{4,3,2,1,0:T(8,128)} %bitcast.6), custom_call_target="tpu_custom_call" | custom-call | tf_op jit(solution)/shard_map/pallas_call | solution.py:431
  254.2 1.2 copy.7
  255.4 1.9 copy.10
  257.3 1.3 copy.11

commit v2 on v1

--- a/solution.py
+++ b/solution.py
@@ -111,7 +111,10 @@
     centres_ref,
     spreads_ref,
     own,
+    expo,
+    step,
     halo,
+    halo_step,
     inter,
     rot,
     uth,
@@ -177,22 +180,28 @@
             device_id_type=MESH,
         )
 
-    def y_copy(t, j, k):
+    def sent(t, k):
+        return own.at[0, k] if t == 0 else step.at[t - 1, k]
+
+    def landed(t, col, z):
+        return halo.at[col, z] if t == 0 else halo_step.at[t - 1, col, z]
+
+    def y_copy(t, j, dx, k):
         slot = -1 if j == 0 else 1
         return remote(
-            own.at[t, k],
-            halo.at[t, column(0, slot), k + 1],
-            y_send.at[t, j, k],
-            y_recv.at[t, j, k],
+            sent(t, k) if dx == 0 else landed(t, column(dx, 0), k + 1),
+            landed(t, column(dx, slot), k + 1),
+            y_send.at[t, j, dx + 1, k],
+            y_recv.at[t, j, dx + 1, k],
             at(0, -slot, 0),
         )
 
     def x_copy(t, i, dy, k):
         slot = -1 if i == 0 else 1
-        src = own.at[t, k] if dy == 0 else halo.at[t, column(0, dy), k + 1]
+        src = sent(t, k) if dy == 0 else landed(t, column(0, dy), k + 1)
         return remote(
             src,
-            halo.at[t, column(slot, dy), k + 1],
+            landed(t, column(slot, dy), k + 1),
             x_send.at[t, i, dy + 1, k],
             x_recv.at[t, i, dy + 1, k],
             at(-slot, 0, 0),
@@ -205,8 +214,8 @@
         else:
             src, dst, target = count, 0, at(0, 0, 1)
         return remote(
-            halo.at[t, col, src],
-            halo.at[t, col, dst],
+            landed(t, col, src),
+            landed(t, col, dst),
             f_send.at[t, f, side],
             f_recv.at[t, f, side],
             target,
@@ -247,11 +256,36 @@
             total = total + axis_slots[t, j]
         return total
 
+    def unpacked(values):
+        flipped = values.T
+        real = jnp.where(row_index < column_index, values, -flipped)
+        return (
+            jnp.where(diagonal, 0.0, real),
+            jnp.where(row_index < column_index, flipped, values),
+        )
+
+    def exponential(change_real, change_imag):
+        change = left_rows(*split(jnp.concatenate([change_real, change_imag], axis=1)))
+        middle = product(
+            change,
+            stacked(0.5 * identity + change_real / 6.0, change_imag / 6.0, False),
+        )
+        exponent = product(
+            change, stacked(identity + middle[:, :width], middle[:, width:], False)
+        )
+        return identity + exponent[:, :width], exponent[:, width:]
+
+    def via_x(k):
+        return lax.rem(k, 2) == 0
+
     def turn(t, k, b):
         dx, dy, dz = OFFSETS[b]
         left = rot[k, b]
-        right = halo.at[t, column(dx, dy), k + 1 + dz]
-        turned = complex_product(left, right[0], right[1])
+        right = landed(t, column(dx, dy), k + 1 + dz)
+        if t == 0:
+            turned = complex_product(left, right[0], right[1])
+        else:
+            turned = complex_product(left, *exponential(*unpacked(right[...])))
         rot[k, b] = turned
         dre[k, b : b + 1, :] = jnp.sum(
             jnp.where(diagonal, turned[:, :width], 0.0), axis=0, keepdims=True
@@ -260,32 +294,47 @@
             jnp.where(diagonal, turned[:, width:], 0.0), axis=0, keepdims=True
         )
 
-    def iteration(t, carry):
+    def iteration(t):
         for k in range(count):
             for j in range(2):
-                y_copy(t, j, k).start()
+                y_copy(t, j, 0, k).start()
             for i in range(2):
                 x_copy(t, i, 0, k).start()
 
         def left_side(k, carry):
-            @pl.when(t == 0)
-            def _():
+            if t == 0:
                 pltpu.make_async_copy(m_ref.at[k], inter.at[k], load_m.at[k]).wait()
-
-            adjoint = jnp.concatenate([own[t, k, 0].T, own[t, k, 1].T], axis=1)
+                adjoint = jnp.concatenate([own[t, k, 0].T, own[t, k, 1].T], axis=1)
+            else:
+                adjoint = jnp.concatenate([expo[k, 0].T, expo[k, 1].T], axis=1)
             uth[...] = left_rows(*split(adjoint))
 
             def one(b, carry):
-                rot[k, b] = product(uth[...], stacked(inter[k, b, 0], inter[k, b, 1], True))
+                if t == 0:
+                    real, imag = inter[k, b, 0], inter[k, b, 1]
+                else:
+                    real, imag = rot[k, b, :, :width], rot[k, b, :, width:]
+                rot[k, b] = product(uth[...], stacked(real, imag, True))
                 return carry
 
             lax.fori_loop(0, NB, one, 0, unroll=3)
             for j in range(2):
-                y_copy(t, j, k).wait_recv()
+                y_copy(t, j, 0, k).wait_recv()
+
+            @pl.when(via_x(k))
+            def _():
                 for i in range(2):
-                    x_copy(t, i, -1 if j == 0 else 1, k).start()
+                    for dy in (-1, 1):
+                        x_copy(t, i, dy, k).start()
+
             for i in range(2):
                 x_copy(t, i, 0, k).wait_recv()
+
+            @pl.when(jnp.logical_not(via_x(k)))
+            def _():
+                for j in range(2):
+                    for dx in (-1, 1):
+                        y_copy(t, j, dx, k).start()
 
             @pl.when(k == 0)
             def _():
@@ -312,9 +361,18 @@
         lax.fori_loop(0, count, faces, 0)
 
         def corners(k, carry):
-            for i in range(2):
-                for dy in (-1, 1):
-                    x_copy(t, i, dy, k).wait_recv()
+            @pl.when(via_x(k))
+            def _():
+                for i in range(2):
+                    for dy in (-1, 1):
+                        x_copy(t, i, dy, k).wait_recv()
+
+            @pl.when(jnp.logical_not(via_x(k)))
+            def _():
+                for j in range(2):
+                    for dx in (-1, 1):
+                        y_copy(t, j, dx, k).wait_recv()
+
             for b in CORNERS:
                 turn(t, k, b)
             return carry
@@ -384,18 +442,13 @@
             scale = STEP_SIZE * 2.0 * WEIGHT
             change_real = scale * (summed_real - summed_real.T)
             change_imag = scale * (summed_imag + summed_imag.T)
-            change = left_rows(*split(jnp.concatenate([change_real, change_imag], axis=1)))
-            middle = product(
-                change,
-                stacked(0.5 * identity + change_real / 6.0, change_imag / 6.0, False),
-            )
-            exponent = product(
-                change, stacked(identity + middle[:, :width], middle[:, width:], False)
-            )
+            expo_real, expo_imag = exponential(change_real, change_imag)
+            if t < ITERS - 1:
+                step[t, k] = jnp.where(row_index < column_index, change_real, change_imag)
+                expo[k, 0] = expo_real
+                expo[k, 1] = expo_imag
             updated = complex_product(
-                jnp.concatenate([own[t, k, 0], own[t, k, 1]], axis=1),
-                identity + exponent[:, :width],
-                exponent[:, width:],
+                jnp.concatenate([own[t, k, 0], own[t, k, 1]], axis=1), expo_real, expo_imag
             )
             own[t + 1, k, 0] = updated[:, :width]
             own[t + 1, k, 1] = updated[:, width:]
@@ -405,19 +458,31 @@
 
         def drain(k, carry):
             for j in range(2):
-                y_copy(t, j, k).wait_send()
+                y_copy(t, j, 0, k).wait_send()
             for i in range(2):
-                for dy in (-1, 0, 1):
-                    x_copy(t, i, dy, k).wait_send()
+                x_copy(t, i, 0, k).wait_send()
+
+            @pl.when(via_x(k))
+            def _():
+                for i in range(2):
+                    for dy in (-1, 1):
+                        x_copy(t, i, dy, k).wait_send()
+
+            @pl.when(jnp.logical_not(via_x(k)))
+            def _():
+                for j in range(2):
+                    for dx in (-1, 1):
+                        y_copy(t, j, dx, k).wait_send()
+
             return carry
 
         lax.fori_loop(0, count, drain, 0)
         for f in range(4):
             for side in range(2):
                 f_copy(t, f, side).wait_send()
-        return carry
-
-    lax.fori_loop(0, ITERS, iteration, 0)
+
+    for t in range(ITERS):
+        iteration(t)
     out_ref[...] = own[ITERS]
 
 
@@ -439,7 +504,10 @@
         out_specs=tuple([pl.BlockSpec(memory_space=pltpu.VMEM)] * 3),
         scratch_shapes=[
             pltpu.VMEM((ITERS + 1, count, 2, width, width), F32),
-            pltpu.VMEM((ITERS, 9, count + 2, 2, width, width), F32),
+            pltpu.VMEM((count, 2, width, width), F32),
+            pltpu.VMEM((ITERS - 1, count, width, width), F32),
+            pltpu.VMEM((9, count + 2, 2, width, width), F32),
+            pltpu.VMEM((ITERS - 1, 9, count + 2, width, width), F32),
             pltpu.VMEM((count, NB, 2, width, width), F32),
             pltpu.VMEM((count, NB, width, 2 * width), F32),
             pltpu.VMEM((width, 6 * width), BF16),
@@ -452,8 +520,8 @@
             pltpu.VMEM((ITERS, nx, 8, width), F32),
             dma,
             dma((count,)),
-            dma((ITERS, 2, count)),
-            dma((ITERS, 2, count)),
+            dma((ITERS, 2, 3, count)),
+            dma((ITERS, 2, 3, count)),
             dma((ITERS, 2, 3, count)),
             dma((ITERS, 2, 3, count)),
             dma((ITERS, 4, 2)),

time: 259 us -> 171 us (0.66)
  Pallas kernels: 254 us -> 166 us
    pallas_call x1, Pallas kernels: 254 us -> 166 us  [body(): pl.pallas_call(functools.partial(kernel, sizes, float(total_points)), out...]
where the time goes in v2:
time: 171 us
  Pallas kernels  166 us (97%)
  local copies, waits for them, and re-layouts  4.41 us (3%)
    pallas_call x1, Pallas kernels, body(): pl.pallas_call(functools.partial(kernel, sizes, float(total_points)), out...  166 us
    unnamed x3, local copies, waits for them, and re-layouts  4.41 us

profile of v2, /device:TPU:0, one launch (start us, length us, event | category | flops | bytes accessed | tf_op | source)
XLA Modules:
  0.0 170.6 jit_solution(9020426627761190942)
XLA Ops:
  0.6 165.6 %shard_map.49 = (f32[4,2,128,128]{3,2,1,0:T(8,128)}, f32[3,3,128]{2,1,0:T(4,128)}, f32[3,1,128]{2,1,0:T(1,128)}) custom-call(f32[4,2,128,128]{3,2,1,0:T(8,128)} %bitcast.8, f32[4,12,2,128,128]{4,3,2,1,0:T(8,128)} %bitcast.6), custom_call_target="tpu_custom_call" | custom-call | tf_op jit(solution)/shard_map/pallas_call | solution.py:496
  166.2 1.2 copy.7
  167.4 1.9 %copy.10 = f32[1,1,4,2,128,128]{5,4,3,2,1,0:T(8,128)} copy(f32[1,1,4,2,128,128]{5,4,3,2,1,0:T(8,128)} %bitcast.7) | data formatting | bytes 1048576
  169.3 1.3 copy.11
